TPU v7x, 32 devices: a whole 2x2x4 slice. The times are simulated.
32 devices in a mesh: pipe: 4 (over z), dp: 4 (over x, core), expert: 2 (over y).
Axes of the slice: x: 2, y: 2, z: 4, core: 2. Of those that a mesh axis runs over, the one named last changes fastest.
Arguments:
- entering: bfloat16 [4, 512, 4096], P('pipe', 'dp', 'expert'), may hold values from -6 to 6
- pending: bfloat16 [4, 512, 4096], P('pipe', 'dp', 'expert'), may hold values from -6 to 6
- stashed_in: bfloat16 [4, 512, 4096], P('pipe', 'dp', 'expert'), may hold values from -6 to 6
- forward_routes: int32 [4, 512, 2], P('pipe', 'dp'), may hold values from 0 to 3, all different within a row; in each aligned block of 128 rows (0 to 127, 128 to 255, ..., all dimensions but the last counted through in order) at most 64 rows name the same one
- backward_routes: int32 [4, 512, 2], P('pipe', 'dp'), may hold values from 0 to 3, all different within a row; in each aligned block of 128 rows (0 to 127, 128 to 255, ..., all dimensions but the last counted through in order) at most 64 rows name the same one
- norm_gains: float32 [4, 4096], P('pipe', 'expert'), may hold values from 0.5 to 1.5
- w_router: bfloat16 [4, 4096, 4], P('pipe', 'expert'), may hold values from -0.09375 to 0.09375
- w_gateup: bfloat16 [4, 4, 4096, 2, 1024], P('pipe', 'dp', None, None, 'expert'), may hold values from -0.09375 to 0.09375
- w_down: bfloat16 [4, 4, 1024, 4096], P('pipe', 'dp', 'expert'), may hold values from -0.1875 to 0.1875
Outputs:
- forward_out: bfloat16 [4, 512, 4096], P('pipe', 'dp', 'expert')
- input_grads: bfloat16 [4, 512, 4096], P('pipe', 'dp', 'expert')
- passed_forward: bfloat16 [4, 512, 4096], P('pipe', 'dp', 'expert')
- passed_backward: bfloat16 [4, 512, 4096], P('pipe', 'dp', 'expert')
- gain_grads: float32 [4, 4096], P('pipe', 'expert')
Inputs may be any that keep to these rules, and one draw needn't show every extreme that they name: `forward_routes`: each row names 2 different experts; in each aligned block of 128 rows (one sequence) every expert is named by exactly 64 rows. `backward_routes`: each row names 2 different experts; in each aligned block of 128 rows (one sequence) every expert is named by exactly 64 rows.
All inputs are finite; a program needn't handle non-finite values.
Results may differ from a plain program's by a relative error of at most 0.015.
Values may be sent and summed in bfloat16 or wider, within the bound.
A program may use at most 64 MiB of HBM per device.

v0:
```python
import jax
import jax.numpy as jnp
from jax import lax
from jax.sharding import PartitionSpec as P

D = 4096


ROUTE_SCALE = 2.827
EPSILON = 1e-05


def shifted(block, axis, distance):
    devices = range(lax.axis_size(axis))
    route = [(i - distance, i) for i in devices if i - distance in devices]
    return lax.ppermute(block, axis, route)


def feature_sum(values):
    return lax.psum(values, "expert")


def normalize(tokens, gain_row):
    values = tokens.astype(jnp.float32)
    squares = feature_sum(jnp.sum(values * values, axis=-1, keepdims=True))
    scaling = lax.rsqrt(squares / D + EPSILON)
    return (values, scaling, (values * scaling * gain_row).astype(jnp.bfloat16))


def gating(moe_in, router, routes):
    experts = router.shape[1]
    logits = feature_sum(jnp.dot(moe_in, router, preferred_element_type=jnp.float32))
    selection = (routes[:, :, None] == jnp.arange(experts, dtype=jnp.int32)[None, None, :]).astype(
        jnp.float32
    )
    chosen = jnp.sum(logits[:, None, :] * selection, axis=-1)
    lifted = jax.nn.sigmoid(chosen)
    lifted_sum = jnp.sum(lifted, axis=-1, keepdims=True)
    return (ROUTE_SCALE * lifted / lifted_sum, lifted, lifted_sum, selection)


def layout(routes, experts):
    capacity = routes.shape[0] * routes.shape[1] // experts
    flattened = routes.reshape(-1)
    member = (flattened[:, None] == jnp.arange(experts, dtype=jnp.int32)[None, :]).astype(jnp.int32)
    before = jnp.cumsum(member, axis=0) - member
    position = jnp.sum(before * member, axis=1)
    destination = flattened * capacity + position
    placing = (
        destination[:, None] == jnp.arange(experts * capacity, dtype=jnp.int32)[None, :]
    ).astype(jnp.bfloat16)
    return (capacity, destination, placing)


def spread(placing, route_rows):
    return jnp.einsum("rc,rd->cd", placing, route_rows, preferred_element_type=jnp.float32).astype(
        jnp.bfloat16
    )


def add_projection(gate_up, segment):
    return jnp.einsum("sxcd,xdkf->sxckf", segment, gate_up, preferred_element_type=jnp.float32)


def run_forward(tokens, routes, gain_row, router, gate_up, down_w):
    length, local_width = tokens.shape
    experts = router.shape[1]
    local_count = gate_up.shape[0]
    values, scaling, moe_in = normalize(tokens, gain_row)
    gate_weights, lifted, lifted_sum, selection = gating(moe_in, router, routes)
    capacity, destination, placing = layout(routes, experts)
    route_rows = jnp.repeat(moe_in, routes.shape[1], axis=0)
    buffer = spread(placing, route_rows).reshape(
        experts // local_count, local_count, capacity, local_width
    )

    def compute(received):
        projected = add_projection(gate_up, lax.all_gather(received, "expert", axis=3, tiled=True))
        gate_pre = projected[:, :, :, 0]
        second = projected[:, :, :, 1]
        inner_act = (jax.nn.silu(gate_pre) * second).astype(jnp.bfloat16)
        partial_value = jnp.einsum(
            "sxcf,xfd->sxcd", inner_act, down_w, preferred_element_type=jnp.float32
        )
        summed = lax.psum_scatter(
            partial_value.astype(jnp.bfloat16), "expert", scatter_dimension=3, tiled=True
        )
        return lax.all_to_all(summed, "dp", split_axis=0, concat_axis=0, tiled=True)

    results = compute(lax.all_to_all(buffer, "dp", split_axis=0, concat_axis=0, tiled=True))
    picked = jnp.take(
        results.reshape(experts * capacity, local_width), destination, axis=0
    ).reshape(length, routes.shape[1], local_width)
    return (values + jnp.sum(gate_weights[:, :, None] * picked.astype(jnp.float32), axis=1)).astype(
        jnp.bfloat16
    )


def run_backward(stashed, incoming, routes, gain_row, router, gate_up, down_w):
    length, local_width = stashed.shape
    experts = router.shape[1]
    local_count = gate_up.shape[0]
    chosen_count = routes.shape[1]
    values, scaling, moe_in = normalize(stashed, gain_row)
    gate_weights, lifted, lifted_sum, selection = gating(moe_in, router, routes)
    capacity, destination, placing = layout(routes, experts)
    slot_shape = (experts // local_count, local_count, capacity, local_width)
    row_buffer = spread(placing, jnp.repeat(moe_in, chosen_count, axis=0)).reshape(slot_shape)
    upstream_buffer = spread(placing, jnp.repeat(incoming, chosen_count, axis=0)).reshape(
        slot_shape
    )

    def compute(received):
        rows_in, up_in = received
        rows_piece = lax.all_gather(rows_in, "expert", axis=3, tiled=True)
        up_piece = lax.all_gather(up_in, "expert", axis=3, tiled=True)
        first_sum = jnp.einsum(
            "sxcd,xdkf->sxckf", rows_piece, gate_up, preferred_element_type=jnp.float32
        )
        second_sum = jnp.einsum(
            "sxcd,xfd->sxcf", up_piece, down_w, preferred_element_type=jnp.float32
        )
        gate_pre = first_sum[:, :, :, 0]
        second = first_sum[:, :, :, 1]
        lifted_act = jax.nn.sigmoid(gate_pre)
        activated = gate_pre * lifted_act
        inner_act = (activated * second).astype(jnp.bfloat16)
        gate_total = feature_sum(
            jnp.sum(inner_act.astype(jnp.float32) * second_sum, axis=-1)
        ).astype(jnp.bfloat16)
        grad_first = (
            second_sum * second * lifted_act * (1.0 + gate_pre * (1.0 - lifted_act))
        ).astype(jnp.bfloat16)
        grad_second = (second_sum * activated).astype(jnp.bfloat16)
        stacked = jnp.stack([grad_first, grad_second], axis=3)
        partial_value = jnp.einsum(
            "sxckf,xdkf->sxcd", stacked, gate_up, preferred_element_type=jnp.float32
        )
        summed = lax.psum_scatter(
            partial_value.astype(jnp.bfloat16), "expert", scatter_dimension=3, tiled=True
        )
        return (
            lax.all_to_all(summed, "dp", split_axis=0, concat_axis=0, tiled=True),
            lax.all_to_all(gate_total, "dp", split_axis=0, concat_axis=0, tiled=True),
        )

    back_rows, back_gate = compute(
        (
            lax.all_to_all(row_buffer, "dp", split_axis=0, concat_axis=0, tiled=True),
            lax.all_to_all(upstream_buffer, "dp", split_axis=0, concat_axis=0, tiled=True),
        )
    )
    back_rows = jnp.take(
        back_rows.reshape(experts * capacity, local_width), destination, axis=0
    ).reshape(length, chosen_count, local_width)
    back_gate = (
        jnp.take(back_gate.reshape(-1), destination, axis=0)
        .reshape(length, chosen_count)
        .astype(jnp.float32)
    )
    moe_cot = jnp.sum(gate_weights[:, :, None] * back_rows.astype(jnp.float32), axis=1).astype(
        jnp.bfloat16
    )
    mixed = jnp.sum(back_gate * lifted, axis=-1, keepdims=True) / lifted_sum
    chosen_cot = ROUTE_SCALE * (back_gate - mixed) / lifted_sum * lifted * (1.0 - lifted)
    logit_cot = jnp.sum(chosen_cot[:, :, None] * selection, axis=1)
    norm_cot = moe_cot.astype(jnp.float32) + jnp.dot(
        logit_cot, router.astype(jnp.float32).T, precision=lax.Precision.HIGHEST
    )
    scaled = norm_cot * gain_row
    inner_product = feature_sum(jnp.sum(scaled * values, axis=-1, keepdims=True))
    token_cot = (
        incoming.astype(jnp.float32)
        + scaling * scaled
        - values * (scaling * scaling * scaling) * inner_product / D
    )
    gain_cot = jnp.sum(norm_cot * values * scaling, axis=0)
    return (token_cot.astype(jnp.bfloat16), gain_cot)


def local(
    entering,
    pending,
    stashed_in,
    forward_routes,
    backward_routes,
    norm_gains,
    w_router,
    w_gateup,
    w_down,
):
    gain_row = norm_gains[0]
    router = w_router[0]
    gate_up = w_gateup[0]
    down_w = w_down[0]
    produced = run_forward(entering[0], forward_routes[0], gain_row, router, gate_up, down_w)
    cotangent, gain_part = run_backward(
        stashed_in[0], pending[0], backward_routes[0], gain_row, router, gate_up, down_w
    )
    passed_forward = shifted(produced, "pipe", 1)
    passed_backward = shifted(cotangent, "pipe", -1)
    gain_total = lax.psum(gain_part, "dp")
    return (
        produced[None],
        cotangent[None],
        passed_forward[None],
        passed_backward[None],
        gain_total[None],
    )


def solution(mesh):
    placed = (
        P("pipe", "dp", "expert"),
        P("pipe", "dp", "expert"),
        P("pipe", "dp", "expert"),
        P("pipe", "dp", None),
        P("pipe", "dp", None),
        P("pipe", "expert"),
        P("pipe", "expert", None),
        P("pipe", "dp", None, None, "expert"),
        P("pipe", "dp", "expert", None),
    )
    return jax.shard_map(
        local,
        mesh=mesh,
        in_specs=placed,
        out_specs=(
            P("pipe", "dp", "expert"),
            P("pipe", "dp", "expert"),
            P("pipe", "dp", "expert"),
            P("pipe", "dp", "expert"),
            P("pipe", "expert"),
        ),
        check_vma=False,
    )
```

profile of v0, /device:TPU:0, one launch (start us, length us, event | category | flops | bytes accessed | tf_op | source)
XLA Modules:
  0.0 331.1 jit_solution(16429123784945353185)
XLA Ops:
  7.2 0.8 copy.106
  8.3 1.2 fusion.46
  9.5 5.9 %psum.51 = f32[128,1]{0,1:T(1,128)S(1)} all-reduce(f32[128,1]{0,1:T(1,128)S(1)} %bitcast.284), channel_id=1, replica_groups=mesh['pipe'=4,'dp'=4,'expert'=2] {'expert'}, use_global_device_ids=true, to_apply=%region_11.13 | all-reduce | flops 128 | bytes 1024 | tf_op jit(solution)/shard_map/psum | solution.py:20
  15.4 1.2 fusion.48
  16.7 0.6 broadcast_in_dim.66
  17.8 1.2 reduce-window.16
  19.4 0.6 convolution_convert_fusion.1
  20.0 17.7 %all_to_all.30 = bf16[4,1,64,2048]{3,2,1,0:T(8,128)(2,1)} all-to-all(bf16[4,1,64,2048]{3,2,1,0:T(8,128)(2,1)S(1)} %bitcast.261), channel_id=1, replica_groups=mesh['pipe'=4,'dp'=4,'expert'=2] {'dp'}, dimensions={0} | all-to-all | bytes 2097152 | tf_op jit(solution)/shard_map/all_to_all | solution.py:149
  37.8 0.6 broadcast_in_dim.65
  39.5 17.6 %all_to_all.31 = bf16[4,1,64,2048]{3,2,1,0:T(8,128)(2,1)} all-to-all(bf16[4,1,64,2048]{3,2,1,0:T(8,128)(2,1)S(1)} %bitcast.262), channel_id=1, replica_groups=mesh['pipe'=4,'dp'=4,'expert'=2] {'dp'}, dimensions={0} | all-to-all | bytes 2097152 | tf_op jit(solution)/shard_map/all_to_all | solution.py:150
  57.1 14.7 %all-gather.8.cloned.1.call-done = bf16[4,1,64,4096]{3,2,0,1:T(8,128)(2,1)} async-done(((bf16[4,1,64,2048]{3,2,0,1:T(8,128)(2,1)}), bf16[4,1,64,4096]{3,2,0,1:T(8,128)(2,1)}) %all-gather.8.cloned.1.call-update) | async-done | bytes 2097168 | tf_op jit(solution)/shard_map/all_gather | solution.py:115
  71.8 6.3 %fusion.26 = f32[4,1,64,2,512]{4,2,0,3,1:T(8,128)S(1)} fusion(bf16[4096,2,512,1]{2,1,0,3:T(2,128)(2,1)} %bitcast.285, bf16[4,1,64,4096]{3,2,0,1:T(8,128)(2,1)} %all-gather.8.cloned.1.call-done), kind=kOutput, calls=%fused_computation.33 | convolution fusion | flops 2147483648 | bytes 11534336 | tf_op jit(solution)/shard_map/sxcd,xdkf->sxckf/dot_general | solution.py:117
  78.1 28.3 %all-gather.6.cloned.1.call-done = bf16[4,1,64,4096]{3,2,0,1:T(8,128)(2,1)} async-done(((bf16[4,1,64,2048]{3,2,0,1:T(8,128)(2,1)}), bf16[4,1,64,4096]{3,2,0,1:T(8,128)(2,1)}) %all-gather.6.cloned.1.call-update) | async-done | bytes 2097168 | tf_op jit(solution)/shard_map/all_gather | solution.py:116
  106.5 4.4 %fusion.82 = (bf16[4,1,64,1,512]{4,2,0,3,1:T(8,128)(2,1)S(1)}, f32[4,64]{1,0:T(4,128)S(1)}, bf16[4,1,64,1,512]{4,2,0,3,1:T(8,128)(2,1)S(1)}) fusion(f32[4,1,64,2,512]{4,2,0,3,1:T(8,128)S(1)} %fusion.26, bf16[1,1,512,4096]{3,2,1,0:T(8,128)(2,1)} %param.19, bf16[4,1,64,4096]{3,2,0,1:T(8,128)(2,1)} %all-gather.6.cloned.1.call-done), kind=kOutput, calls=%fused_computation.89 | convolution fusion | flops 1076100864 | bytes 7865344 | tf_op jit(solution)/shard_map/sxcd,xfd->sxcf/dot_general | solution.py:120
  110.8 7.1 %fusion.14 = bf16[4,1,64,4096]{3,2,0,1:T(8,128)(2,1)} fusion(bf16[4096,2,512,1]{2,1,0,3:T(2,128)(2,1)} %bitcast.286, bf16[4,1,64,1,512]{4,2,0,3,1:T(8,128)(2,1)S(1)} %get-tuple-element.25, bf16[4,1,64,1,512]{4,2,0,3,1:T(8,128)(2,1)S(1)} %get-tuple-element.23), kind=kOutput, calls=%fused_computation.14 | convolution fusion | flops 2148794368 | bytes 11010048 | tf_op jit(solution)/shard_map/sxckf,xdkf->sxcd/dot_general | solution.py:136
  119.4 1.2 reduce-window.14
  121.6 8.1 %all-reduce.1 = (f32[128,1]{0,1:T(1,128)S(1)}, f32[128,4]{0,1:T(4,128)S(1)}, bf16[4,1,64]{2,1,0:T(2,128)(2,1)}) all-reduce(f32[128,1]{0,1:T(1,128)S(1)} %bitcast.282, f32[128,4]{0,1:T(4,128)S(1)} %fusion.69, f32[4,1,64]{2,1,0:T(1,128)S(1)} %bitcast.283), channel_id=1, replica_groups=mesh['pipe'=4,'dp'=4,'expert'=2] {'expert'}, use_global_device_ids=true, to_apply=%region_1.0 | all-reduce | flops 896 | bytes 6656 | tf_op jit(solution)/shard_map/psum | solution.py:20
  129.7 3.2 all-to-all-start.5
  132.9 3.6 %all-to-all-done.5 = bf16[4,1,64]{2,1,0:T(2,128)(2,1)S(1)} async-done(((bf16[4,1,64]{2,1,0:T(2,128)(2,1)}), bf16[4,1,64]{2,1,0:T(2,128)(2,1)S(1)}, u32[]{:S(2)}, u32[]{:S(2)}) %all-to-all-start.5) | async-done | bytes 544 | tf_op jit(solution)/shard_map/all_to_all | solution.py:144
  136.6 13.9 %reduce-scatter.5.cloned.1.call-done = bf16[4,1,64,2048]{3,2,0,1:T(8,128)(2,1)} async-done(((bf16[4,1,64,4096]{3,2,0,1:T(8,128)(2,1)}), bf16[4,1,64,2048]{3,2,0,1:T(8,128)(2,1)}) %reduce-scatter.5.cloned.1.call-update) | async-done | bytes 1048592 | tf_op jit(solution)/shard_map/reduce_scatter | solution.py:139
  150.5 3.5 %all-to-all-start.4 = ((bf16[4,1,64,2048]{3,2,1,0:T(8,128)(2,1)}), bf16[4,1,64,2048]{3,2,1,0:T(8,128)(2,1)S(1)}, u32[]{:S(2)}, u32[]{:S(2)}) async-start(bf16[4,1,64,2048]{3,2,1,0:T(8,128)(2,1)} %bitcast.265), calls=%async_computation.6 | async-start | bytes 2097152 | tf_op jit(solution)/shard_map/all_to_all | solution.py:143
  154.6 1.9 gather_fusion
  157.0 11.4 %all-to-all-done.4 = bf16[4,1,64,2048]{3,2,1,0:T(8,128)(2,1)S(1)} async-done(((bf16[4,1,64,2048]{3,2,1,0:T(8,128)(2,1)}), bf16[4,1,64,2048]{3,2,1,0:T(8,128)(2,1)S(1)}, u32[]{:S(2)}, u32[]{:S(2)}) %all-to-all-start.4) | async-done | bytes 1048608 | tf_op jit(solution)/shard_map/all_to_all | solution.py:143
  168.4 2.3 gather_fusion.2
  170.7 1.4 select_convert_fusion
  172.2 2.3 reshape.445
  174.5 4.8 %multiply_reduce_fusion = bf16[128,2048]{1,0:T(8,128)(2,1)S(1)} fusion(f32[128,2,2048]{2,1,0:T(2,128)} %reshape.445, f32[128,2]{1,0:T(8,128)S(1)} %copy.105), kind=kLoop, calls=%fused_computation.25 | loop fusion | flops 786432 | bytes 2622464 | tf_op jit(solution)/shard_map/reduce_sum | solution.py:161
  179.3 1.0 fusion.55
  180.3 4.9 %all-reduce = (f32[128,4]{0,1:T(4,128)S(1)}, f32[128]{0:T(128)S(1)}) all-reduce(f32[128,4]{0,1:T(4,128)S(1)} %fusion.66, f32[128]{0:T(128)S(1)} %get-tuple-element.7), channel_id=1, replica_groups=mesh['pipe'=4,'dp'=4,'expert'=2] {'expert'}, use_global_device_ids=true, to_apply=%region_2.0 | all-reduce | flops 640 | bytes 5120 | tf_op jit(solution)/shard_map/psum | solution.py:20
  185.8 0.6 broadcast_in_dim.36
  187.4 17.6 %all_to_all.32 = bf16[4,1,64,2048]{3,2,1,0:T(8,128)(2,1)} all-to-all(bf16[4,1,64,2048]{3,2,1,0:T(8,128)(2,1)S(1)} %bitcast.263), channel_id=1, replica_groups=mesh['pipe'=4,'dp'=4,'expert'=2] {'dp'}, dimensions={0} | all-to-all | bytes 2097152 | tf_op jit(solution)/shard_map/all_to_all | solution.py:90
  205.1 32.3 %all-gather.4.cloned.1.call-done = bf16[4,1,64,4096]{3,2,0,1:T(8,128)(2,1)} async-done(((bf16[4,1,64,2048]{3,2,0,1:T(8,128)(2,1)}), bf16[4,1,64,4096]{3,2,0,1:T(8,128)(2,1)}) %all-gather.4.cloned.1.call-update) | async-done | bytes 2097168 | tf_op jit(solution)/shard_map/all_gather | solution.py:78
  237.4 6.5 %fusion.31 = f32[4,1,64,2,512]{4,2,3,0,1:T(8,128)S(1)} fusion(bf16[4096,2,512]{2,1,0:T(2,128)(2,1)} %bitcast.287, bf16[4,1,64,4096]{3,2,0,1:T(8,128)(2,1)} %all-gather.4.cloned.1.call-done), kind=kOutput, calls=%fused_computation.34 | convolution fusion | flops 2147483648 | bytes 11534336 | tf_op jit(solution)/shard_map/sxcd,xdkf->sxckf/dot_general | solution.py:62
  243.9 2.7 fusion.13
  246.6 32.1 %reduce-scatter.3.cloned.1.call-done = bf16[4,1,64,2048]{3,2,0,1:T(8,128)(2,1)} async-done(((bf16[4,1,64,4096]{3,2,0,1:T(8,128)(2,1)}), bf16[4,1,64,2048]{3,2,0,1:T(8,128)(2,1)}) %reduce-scatter.3.cloned.1.call-update) | async-done | bytes 1048592 | tf_op jit(solution)/shard_map/reduce_scatter | solution.py:85
  278.6 3.5 %all-to-all-start.1 = ((bf16[4,1,64,2048]{3,2,1,0:T(8,128)(2,1)}), bf16[4,1,64,2048]{3,2,1,0:T(8,128)(2,1)S(1)}, u32[]{:S(2)}, u32[]{:S(2)}) async-start(bf16[4,1,64,2048]{3,2,1,0:T(8,128)(2,1)} %bitcast.266), calls=%async_computation.2 | async-start | bytes 2097152 | tf_op jit(solution)/shard_map/all_to_all | solution.py:88
  282.4 1.5 collective-permute-start.1
  283.9 12.7 %all-to-all-done.1 = bf16[4,1,64,2048]{3,2,1,0:T(8,128)(2,1)S(1)} async-done(((bf16[4,1,64,2048]{3,2,1,0:T(8,128)(2,1)}), bf16[4,1,64,2048]{3,2,1,0:T(8,128)(2,1)S(1)}, u32[]{:S(2)}, u32[]{:S(2)}) %all-to-all-start.1) | async-done | bytes 1048608 | tf_op jit(solution)/shard_map/all_to_all | solution.py:88
  296.5 2.3 gather_fusion.1
  298.9 1.4 select_convert_fusion.1
  300.3 2.3 reshape.443
  302.6 4.7 %multiply_reduce_fusion.1 = f32[128,2048]{1,0:T(8,128)S(1)} fusion(f32[128,2,2048]{2,1,0:T(2,128)} %reshape.443, f32[128,2]{1,0:T(8,128)S(1)} %copy.96), kind=kLoop, calls=%fused_computation.26 | loop fusion | flops 786432 | bytes 3146752 | tf_op jit(solution)/shard_map/reduce_sum | solution.py:94
  307.5 3.4 %collective-permute-start = (bf16[128,2048]{1,0:T(8,128)(2,1)S(1)}, bf16[128,2048]{1,0:T(8,128)(2,1)S(1)}, u32[]{:S(2)}, u32[]{:S(2)}) collective-permute-start(bf16[128,2048]{1,0:T(8,128)(2,1)S(1)} %fusion.61), channel_id=1, source_target_pairs={{0,8},{8,16},{16,24},{1,9},{9,17},{17,25},{2,10},{10,18},{18,26},{... | collective-permute-start | bytes 1572872 | tf_op jit(solution)/shard_map/ppermute | solution.py:16
  310.9 6.5 %psum.55 = f32[1,2048]{1,0:T(1,128)} all-reduce(f32[1,2048]{1,0:T(1,128)S(1)} %bitcast.277), channel_id=1, replica_groups=mesh['pipe'=4,'dp'=4,'expert'=2] {'dp'}, use_global_device_ids=true, to_apply=%region_27.29 | all-reduce | flops 2048 | bytes 16384 | tf_op jit(solution)/shard_map/psum | solution.py:202
  317.4 0.9 fusion.64
  318.3 3.6 %collective-permute-done = bf16[128,2048]{1,0:T(8,128)(2,1)S(1)} collective-permute-done((bf16[128,2048]{1,0:T(8,128)(2,1)S(1)}, bf16[128,2048]{1,0:T(8,128)(2,1)S(1)}, u32[]{:S(2)}, u32[]{:S(2)}) %collective-permute-start) | collective-permute-done | bytes 524320 | tf_op jit(solution)/shard_map/ppermute | solution.py:16
  321.9 0.8 copy.151
  322.7 1.9 copy.152
  (91 shorter events, 7.6 us)
Async XLA Ops:
  7.2 114.1 %copy-start = (bf16[1,2048,4]{1,2,0:T(4,128)(2,1)S(1)}, bf16[1,2048,4]{1,2,0:T(4,128)(2,1)}, u32[]{:S(2)}) copy-start(bf16[1,2048,4]{1,2,0:T(4,128)(2,1)} %param.17) | copy-start | bytes 49156
  7.2 64.6 %all-gather.8.cloned.1.call-start = ((), (), s32[]{:S(2)}) async-start(), calls=%async_computation.11 | async-start | bytes 3145728 | tf_op jit(solution)/shard_map/all_gather | solution.py:115
  20.0 17.8 %copy-start.3 = (bf16[1,128,2048]{2,1,0:T(8,128)(2,1)S(1)}, bf16[1,128,2048]{2,1,0:T(8,128)(2,1)}, u32[]{:S(2)}) copy-start(bf16[1,128,2048]{2,1,0:T(8,128)(2,1)} %param.12) | copy-start | bytes 1572868
  37.8 68.7 %all-gather.6.cloned.1.call-start = ((), (), s32[]{:S(2)}) async-start(), calls=%async_computation.10 | async-start | bytes 3145728 | tf_op jit(solution)/shard_map/all_gather | solution.py:116
  57.1 93.4 %reduce-scatter.5.cloned.1.call-start = ((), (), s32[]{:S(2)}) async-start(), calls=%async_computation.12 | async-start | bytes 3145728 | tf_op jit(solution)/shard_map/reduce_scatter | solution.py:139
  118.0 0.7 copy-start.8
  118.0 1.1 copy-start.7
  118.0 3.1 copy-start.1
  118.0 3.3 copy-start.2
  118.0 3.3 %copy-start.6 = (f32[1,2048]{1,0:T(1,128)S(1)}, f32[1,2048]{1,0:T(1,128)}, u32[]{:S(2)}) copy-start(f32[1,2048]{1,0:T(1,128)} %param.16) | copy-start | bytes 24580
  129.7 6.9 %all-to-all-start.5 = ((bf16[4,1,64]{2,1,0:T(2,128)(2,1)}), bf16[4,1,64]{2,1,0:T(2,128)(2,1)S(1)}, u32[]{:S(2)}, u32[]{:S(2)}) async-start(bf16[4,1,64]{2,1,0:T(2,128)(2,1)} %get-tuple-element.14), calls=%async_computation.7 | async-start | bytes 4096 | tf_op jit(solution)/shard_map/all_to_all | solution.py:144
  150.5 17.9 %all-to-all-start.4 = ((bf16[4,1,64,2048]{3,2,1,0:T(8,128)(2,1)}), bf16[4,1,64,2048]{3,2,1,0:T(8,128)(2,1)S(1)}, u32[]{:S(2)}, u32[]{:S(2)}) async-start(bf16[4,1,64,2048]{3,2,1,0:T(8,128)(2,1)} %bitcast.265), calls=%async_computation.6 | async-start | bytes 2097152 | tf_op jit(solution)/shard_map/all_to_all | solution.py:143
  154.0 83.4 %all-gather.4.cloned.1.call-start = ((), (), s32[]{:S(2)}) async-start(), calls=%async_computation.8 | async-start | bytes 3145728 | tf_op jit(solution)/shard_map/all_gather | solution.py:78
  174.5 10.8 %copy-start.4 = (bf16[1,128,2048]{2,1,0:T(8,128)(2,1)S(1)}, bf16[1,128,2048]{2,1,0:T(8,128)(2,1)}, u32[]{:S(2)}) copy-start(bf16[1,128,2048]{2,1,0:T(8,128)(2,1)} %param.12) | copy-start | bytes 1572868
  185.7 96.6 %copy-start.5 = (bf16[128,2048]{1,0:T(8,128)(2,1)}, bf16[128,2048]{1,0:T(8,128)(2,1)S(1)}, u32[]{:S(2)}) copy-start(bf16[128,2048]{1,0:T(8,128)(2,1)S(1)} %get-tuple-element.26) | copy-start | bytes 1572868
  205.0 73.6 %reduce-scatter.3.cloned.1.call-start = ((), (), s32[]{:S(2)}) async-start(), calls=%async_computation.9 | async-start | bytes 3145728 | tf_op jit(solution)/shard_map/reduce_scatter | solution.py:85
  237.4 6.5 %copy-start.9 = (bf16[1,1,512,4096]{3,2,1,0:T(8,128)(2,1)S(1)}, bf16[1,1,512,4096]{3,2,1,0:T(8,128)(2,1)}, u32[]{:S(2)}) copy-start(bf16[1,1,512,4096]{3,2,1,0:T(8,128)(2,1)} %param.19) | copy-start | bytes 12582916
  278.6 17.9 %all-to-all-start.1 = ((bf16[4,1,64,2048]{3,2,1,0:T(8,128)(2,1)}), bf16[4,1,64,2048]{3,2,1,0:T(8,128)(2,1)S(1)}, u32[]{:S(2)}, u32[]{:S(2)}) async-start(bf16[4,1,64,2048]{3,2,1,0:T(8,128)(2,1)} %bitcast.266), calls=%async_computation.2 | async-start | bytes 2097152 | tf_op jit(solution)/shard_map/all_to_all | solution.py:88
  282.4 35.0 %collective-permute-start.1 = (bf16[128,2048]{1,0:T(8,128)(2,1)S(1)}, bf16[128,2048]{1,0:T(8,128)(2,1)}, u32[]{:S(2)}, u32[]{:S(2)}) collective-permute-start(bf16[128,2048]{1,0:T(8,128)(2,1)S(1)} %get-tuple-element.26), channel_id=1, source_target_pairs={{8,0},{16,8},{24,16},{9,1},{17,9},{25,17},{10,2},{18,10},{26,18},{... | collective-permute-start | bytes 1572872 | tf_op jit(solution)/shard_map/ppermute | solution.py:16
  307.5 14.4 %collective-permute-start = (bf16[128,2048]{1,0:T(8,128)(2,1)S(1)}, bf16[128,2048]{1,0:T(8,128)(2,1)S(1)}, u32[]{:S(2)}, u32[]{:S(2)}) collective-permute-start(bf16[128,2048]{1,0:T(8,128)(2,1)S(1)} %fusion.61), channel_id=1, source_target_pairs={{0,8},{8,16},{16,24},{1,9},{9,17},{17,25},{2,10},{10,18},{18,26},{... | collective-permute-start | bytes 1572872 | tf_op jit(solution)/shard_map/ppermute | solution.py:16
Sparse Core Ops, SparseCore 0:
  37.9 33.8 all-gather.7
  73.3 33.0 all-gather.5
  118.1 32.2 reduce-scatter.4
  205.1 32.1 all-gather.3
  246.7 31.8 reduce-scatter.2
where the time goes:
time: 332 us; the launch traced here: 331 us
  waiting for transfers between devices  153 us (46%)
  blocking collectives  78.3 us (24%)
  matrix products  30.2 us (9%)
  local copies, waits for them, and re-layouts  20.6 us (6%)
  other arithmetic  19.6 us (6%)
  starting transfers between devices  15.6 us (5%)
  between operations  14.2 us (4%)
    reduce_scatter x2, waiting for transfers between devices, compute(): lax.psum_scatter(partial_value.astype(jnp.bfloat16), 'expert', scatter_di...  45.9 us
    all_gather x1, waiting for transfers between devices, compute(): lax.all_gather(received, 'expert', axis=3, tiled=True)  32.3 us
    all_gather x1, waiting for transfers between devices, compute(): up_piece = lax.all_gather(up_in, 'expert', axis=3, tiled=True)  28.3 us
    psum x3, blocking collectives, feature_sum(): return lax.psum(values, 'expert')  18.9 us
    all_to_all x1, blocking collectives, run_backward(): lax.all_to_all(row_buffer, 'dp', split_axis=0, concat_axis=0, tiled=True)  17.7 us
    all_to_all x1, blocking collectives, run_forward(): lax.all_to_all(buffer, 'dp', split_axis=0, concat_axis=0, tiled=True)  17.6 us
    all_to_all x1, blocking collectives, run_backward(): lax.all_to_all(upstream_buffer, 'dp', split_axis=0, concat_axis=0, tiled=...  17.6 us
    all_gather x1, waiting for transfers between devices, compute(): rows_piece = lax.all_gather(rows_in, 'expert', axis=3, tiled=True)  14.7 us
  transfers between devices with their start and end apart: 10, of which 9 were waited for; matrix products, arithmetic and copies ran while one was open for 8% of the time, Pallas kernels for 0%

commit v1 on v0

v1 whole, which is shorter than its diff:
```python
import functools

import jax
import jax.numpy as jnp
from jax import lax
from jax.experimental import pallas as pl
from jax.experimental.pallas import tpu as pltpu
from jax.sharding import PartitionSpec as P

ROUTE_SCALE = 2.827
EPSILON = 1e-05
F32 = jnp.float32
BF16 = jnp.bfloat16
MESH = pl.DeviceIdType.MESH
NT = (((1,), (1,)), ((), ()))
GAIN_ROW = 7


def nt(a, b):
    return lax.dot_general(a, b, NT, preferred_element_type=F32)


def nn(a, b):
    return jnp.dot(a, b, preferred_element_type=F32)


def split(v):
    hi = v.astype(BF16)
    return hi, (v - hi.astype(F32)).astype(BF16)


def kernel(
    cfg,
    xb_in, gy_in, xf_in, routes_in, small_in, wgu_in, wd_in,
    fo, ig, pf, pb, gg,
    g_all, rt, sm, wgu, wd, rows_x, rows_g, acc_a, acc_b, acc_w, inner, grad,
    ret_send, ret, comb_send, comb, own, hot, wts, gs, gr, dm, ip, gpart, r_tok, rpad,
    send_sem, recv_sem, local_sem,
):
    NP, ND, NY, TOK, DL, FFL, K, E, CAP = cfg
    HT = TOK // 2
    W = min(256, DL)
    tiles = DL // W
    NSLOT = E * CAP
    D = DL * NY
    p, d, y = lax.axis_index("pipe"), lax.axis_index("dp"), lax.axis_index("expert")
    core = lax.rem(d, 2)
    mate = d + 1 - 2 * core
    across = [lax.rem(d + 2 * o, ND) for o in range(1, ND // 2)]
    others_y = [lax.rem(y + o, NY) for o in range(1, NY)]
    others_d = [lax.rem(d + o, ND) for o in range(1, ND)]
    up, down = lax.rem(p + 1, NP), lax.rem(p + NP - 1, NP)

    counter = {"s": 0, "r": 0, "l": 0}
    pending = []

    def remote(src, dst, r_index, where):
        i = counter["s"]
        counter["s"] += 1
        c = pltpu.make_async_remote_copy(
            src_ref=src, dst_ref=dst, send_sem=send_sem.at[i], recv_sem=recv_sem.at[r_index],
            device_id=where, device_id_type=MESH,
        )
        c.start()
        pending.append(c)

    def arrived(ref, r_index):
        pltpu.make_async_remote_copy(
            src_ref=ref, dst_ref=ref, send_sem=send_sem.at[0], recv_sem=recv_sem.at[r_index],
            device_id=(p, d, y), device_id_type=MESH,
        ).wait_recv()

    def local(src, dst):
        i = counter["l"]
        counter["l"] += 1
        c = pltpu.make_async_copy(src, dst, local_sem.at[i])
        c.start()
        return c

    def block(n):
        base = counter["r"]
        counter["r"] += n
        return base

    first = [local(src, g_all.at[t, d, y]) for t, src in enumerate((xb_in, gy_in, xf_in))]
    first.append(local(routes_in, rt.at[d]))
    first.append(local(small_in, sm.at[y]))
    weights = [local(wgu_in.at[k, pl.ds(j * DL, DL)], wgu.at[k, j]) for k in range(2) for j in range(NY)]
    weights += [local(wd_in.at[:, pl.ds(j * DL, DL)], wd.at[j]) for j in range(NY)]

    barrier = pltpu.get_barrier_semaphore()
    for o in range(ND):
        for v in range(NY):
            if o or v:
                pl.semaphore_signal(
                    barrier, inc=1, device_id=(p, lax.rem(d + o, ND), lax.rem(y + v, NY)), device_id_type=MESH
                )
    pl.semaphore_signal(barrier, inc=1, device_id=(up, d, y), device_id_type=MESH)
    pl.semaphore_signal(barrier, inc=1, device_id=(down, d, y), device_id_type=MESH)
    pl.semaphore_wait(barrier, ND * NY + 1)
    for c in first:
        c.wait()

    gbase = block(3 * ND * NY * 2)

    def piece(t, dd, yy, h):
        return g_all.at[t, dd, yy, pl.ds(h * HT, HT)]

    def gsem(t, dd, yy, h):
        return gbase + ((t * ND + dd) * NY + yy) * 2 + h

    def gsend(t, dd, yy, h, where):
        ref = piece(t, dd, yy, h)
        remote(ref, ref, gsem(t, dd, yy, h), where)

    def gwait(t, dd, yy, h):
        arrived(piece(t, dd, yy, h), gsem(t, dd, yy, h))

    def send_own(t):
        for i in range(2):
            for x in across:
                gsend(t, d, y, i, (p, x, y))
            for v in others_y:
                gsend(t, d, y, 1 - i, (p, d, v))
        for i in range(2):
            gsend(t, d, y, i, (p, mate, y))

    def relay(t):
        for i in range(2):
            for x in across:
                gwait(t, x, y, i)
                if i == 0:
                    for v in others_y:
                        gsend(t, x, y, 0, (p, d, v))
                gsend(t, x, y, i, (p, mate, y))
            for v in others_y:
                gwait(t, d, v, 1 - i)
                if i == 0:
                    for x in across:
                        gsend(t, d, v, 1, (p, x, y))
                gsend(t, d, v, 1 - i, (p, mate, y))

    def finish(t):
        for x in across:
            for v in others_y:
                for h in range(2):
                    gwait(t, x, v, h)
                    gsend(t, x, v, h, (p, mate, y))
        for dd in [mate] + [lax.rem(mate + 2 * o, ND) for o in range(1, ND // 2)]:
            for v in range(NY):
                for h in range(2):
                    gwait(t, dd, v, h)

    rbase, sbase = block(ND), block(NY)
    for s in others_d:
        remote(rt.at[d], rt.at[d], rbase + d, (p, s, y))
    for v in others_y:
        remote(sm.at[y], sm.at[y], sbase + y, (p, d, v))
    send_own(0)
    send_own(1)
    for s in others_d:
        arrived(rt.at[s], rbase + s)
    for v in others_y:
        arrived(sm.at[v], sbase + v)

    before = (
        lax.broadcasted_iota(jnp.int32, (TOK, TOK), 0) < lax.broadcasted_iota(jnp.int32, (TOK, TOK), 1)
    ).astype(F32).astype(BF16)
    row8 = lax.broadcasted_iota(jnp.int32, (8, TOK), 0)
    slot = lax.broadcasted_iota(jnp.int32, (CAP, TOK), 0).astype(F32)

    def one_hot(member_row, pos_row):
        return jnp.where(slot == pos_row, member_row, 0.0)

    def expert_hot(s, base):
        picks = rt[s]
        member = jnp.zeros((8, TOK), F32)
        for k in range(K):
            member += (picks[base + k : base + k + 1, :] == d).astype(F32)
        pos = nn(member.astype(BF16), before)
        return one_hot(member[0:1, :], pos[0:1, :]).astype(BF16)

    def dispatch(t, base, rows, scaled):
        def body(s, _):
            pick = expert_hot(s, base)
            where = pl.ds(pl.multiple_of(s * CAP, CAP), CAP)
            total = jnp.zeros((CAP, 1), F32)
            for j in range(NY):
                def step(i, tot, j=j):
                    cols = pl.ds(pl.multiple_of(i * W, W), W)
                    part = nn(pick, g_all[t, s, j, :, cols])
                    rows[j, where, cols] = part.astype(BF16)
                    return tot + jnp.sum(part * part, axis=-1, keepdims=True)

                total = lax.fori_loop(0, tiles, step, total)
            if scaled:
                scaling = lax.rsqrt(total / D + EPSILON)
                for j in range(NY):
                    def norm(i, c, j=j):
                        cols = pl.ds(pl.multiple_of(i * W, W), W)
                        v = rows[j, where, cols].astype(F32) * scaling * sm[j, GAIN_ROW : GAIN_ROW + 1, cols]
                        rows[j, where, cols] = v.astype(BF16)
                        return c

                    lax.fori_loop(0, tiles, norm, 0)
            return 0

        lax.fori_loop(0, ND, body, 0)

    def project_up():
        acc_a[...] = jnp.zeros_like(acc_a)
        acc_b[...] = jnp.zeros_like(acc_b)
        KT = min(512, DL)
        for j in range(NY):
            def body(i, c, j=j):
                ks = pl.ds(pl.multiple_of(i * KT, KT), KT)
                lhs = rows_x[j, :, ks]
                acc_a[...] += nn(lhs, wgu[0, j, ks, :])
                acc_b[...] += nn(lhs, wgu[1, j, ks, :])
                return c

            lax.fori_loop(0, DL // KT, body, 0)

    def project_w():
        acc_w[...] = jnp.zeros_like(acc_w)
        KT = min(512, DL)
        for j in range(NY):
            def body(i, c, j=j):
                ks = pl.ds(pl.multiple_of(i * KT, KT), KT)
                acc_w[...] += nt(rows_g[j, :, ks], wd[j, :, ks])
                return c

            lax.fori_loop(0, DL // KT, body, 0)

    def owner(t, base, u):
        def squares(j, tot):
            def step(i, tt):
                v = g_all[t, d, j, :, pl.ds(pl.multiple_of(i * W, W), W)].astype(F32)
                return tt + jnp.sum(v * v, axis=-1, keepdims=True)

            return lax.fori_loop(0, tiles, step, tot)

        total = lax.fori_loop(0, NY, squares, jnp.zeros((TOK, 1), F32))
        scaling = lax.rsqrt(total / D + EPSILON)

        def logit(j, acc):
            def step(i, a):
                cols = pl.ds(pl.multiple_of(i * W, W), W)
                v = g_all[t, d, j, :, cols].astype(F32) * scaling * sm[j, GAIN_ROW : GAIN_ROW + 1, cols]
                return a + nt(sm[j, :, cols].astype(BF16), v.astype(BF16))

            return lax.fori_loop(0, tiles, step, acc)

        logits = lax.fori_loop(0, NY, logit, jnp.zeros((8, TOK), F32))
        picks = rt[d]
        sel = jnp.zeros((8, TOK), F32)
        for k in range(K):
            sel += (picks[base + k : base + k + 1, :] == row8).astype(F32)
        pos = nn(sel.astype(BF16), before)
        sg = jnp.where(sel > 0.5, jax.nn.sigmoid(logits), 0.0)
        total_sg = jnp.sum(sg, axis=0, keepdims=True)
        gate = ROUTE_SCALE * sg / total_sg
        weighted = []
        for e in range(E):
            h = one_hot(sel[e : e + 1, :], pos[e : e + 1, :])
            hot[u, e] = h.astype(BF16)
            weighted.append(h * gate[e : e + 1, :])
        g = jnp.transpose(jnp.concatenate(weighted, axis=0))
        hi, lo = split(g)
        wts[u, 0] = hi
        wts[u, 1] = lo
        return scaling, sel, sg, total_sg

    retbase = [block(NY * ND) for _ in range(2)]
    cbase = [block(NY) for _ in range(2)]
    gcbase, ipbase, gpbase, zbase = block(ND * NY), block(NY), block(ND), block(2)

    def chunk_of(i):
        return lax.rem(y + 1 + i, NY)

    def produce(u, i, make):
        j = chunk_of(i)

        def body(n, c):
            cols = pl.ds(pl.multiple_of(n * W, W), W)
            ret_send[u, j, :, :, cols] = make(j, cols).astype(BF16).reshape(ND, CAP, W)
            return c

        lax.fori_loop(0, tiles, body, 0)
        for s in others_d:
            remote(ret_send.at[u, j, s], ret.at[u, j, d], retbase[u] + j * ND + d, (p, s, y))
        return local(ret_send.at[u, j, d], ret.at[u, j, d])

    def combine(u, i, kept):
        j = chunk_of(i)
        for s in others_d:
            arrived(ret.at[u, j, s], retbase[u] + j * ND + s)
        kept.wait()

        def body(n, c):
            cols = pl.ds(pl.multiple_of(n * W, W), W)
            r = ret[u, j, :, :, cols].reshape(NSLOT, W)
            v = nn(wts[u, 0], r) + nn(wts[u, 1], r)
            if i < NY - 1:
                comb_send[u, j, :, cols] = v.astype(BF16)
            else:
                own[:, cols] = v
            return c

        lax.fori_loop(0, tiles, body, 0)
        if i < NY - 1:
            remote(comb_send.at[u, j], comb.at[u, y], cbase[u] + y, (p, d, j))

    def combined(u, cols):
        v = own[:, cols]
        for w in others_y:
            v = v + comb[u, w, :, cols].astype(F32)
        return v

    relay(0)
    relay(1)
    send_own(2)
    r_b, sel_b, sg_b, sum_b = owner(0, K, 0)
    r_tok[...] = jnp.broadcast_to(r_b, r_tok.shape)
    finish(0)
    dispatch(0, K, rows_x, True)
    for c in weights:
        c.wait()
    project_up()
    finish(1)
    dispatch(1, K, rows_g, False)
    project_w()
    ones8 = jnp.ones((8, FFL), BF16)

    def activate(s, c):
        where = pl.ds(pl.multiple_of(s * CAP, CAP), CAP)
        a, b, w = acc_a[where, :], acc_b[where, :], acc_w[where, :]
        sa = jax.nn.sigmoid(a)
        act = a * sa
        prod = (act * b).astype(BF16).astype(F32) * w
        hi, lo = split(prod)
        gs[s] = nt(ones8, hi) + nt(ones8, lo)
        grad[0, where, :] = (w * b * sa * (1.0 + a * (1.0 - sa))).astype(BF16)
        grad[1, where, :] = (w * act).astype(BF16)
        return c

    lax.fori_loop(0, ND, activate, 0)
    for o in range(ND):
        for v in range(NY):
            if o or v:
                s = lax.rem(d + o, ND)
                remote(gs.at[s], gr.at[d, y], gcbase + d * NY + y, (p, s, lax.rem(y + v, NY)))
    kept_gc = local(gs.at[d], gr.at[d, y])

    def back_rows(j, cols):
        return nt(grad[0], wgu[0, j, cols, :]) + nt(grad[1], wgu[1, j, cols, :])

    relayed = False
    kept_b = []
    for i in range(NY):
        kept_b.append(produce(0, i, back_rows))
        if i == 0:
            relay(2)
    owner(2, 0, 1)
    finish(2)
    dispatch(2, 0, rows_x, True)
    project_up()

    def act_forward(s, c):
        where = pl.ds(pl.multiple_of(s * CAP, CAP), CAP)
        a, b = acc_a[where, :], acc_b[where, :]
        inner[where, :] = (a * jax.nn.sigmoid(a) * b).astype(BF16)
        return c

    lax.fori_loop(0, ND, act_forward, 0)

    def forward_rows(j, cols):
        return nn(inner[...], wd[j, :, cols])

    kept_f = []
    for i in range(NY):
        combine(0, i, kept_b[i])
        kept_f.append(produce(1, i, forward_rows))

    kept_gc.wait()
    for o in range(ND):
        for v in range(NY):
            if o or v:
                s, w = lax.rem(d + o, ND), lax.rem(y + v, NY)
                arrived(gr.at[s, w], gcbase + s * NY + w)
    gc = jnp.zeros((8, TOK), F32)
    for e in range(E):
        t = gr[e, 0]
        for v in range(1, NY):
            t = t + gr[e, v]
        gc = gc + jnp.where(row8 == e, nn(t.astype(BF16), hot[0, e]), 0.0)
    mixed = jnp.sum(gc * sg_b, axis=0, keepdims=True) / sum_b
    dl = jnp.where(sel_b > 0.5, ROUTE_SCALE * (gc - mixed) / sum_b * sg_b * (1.0 - sg_b), 0.0)
    dl_hi, dl_lo = split(jnp.transpose(jnp.concatenate([dl, jnp.zeros((TOK - 8, TOK), F32)], axis=0)))
    rpad[...] = jnp.zeros_like(rpad)
    rpad[0:8, :] = sm[y]
    for w in others_y:
        arrived(comb.at[0, w], cbase[0] + w)

    def tail_one(n, tot):
        cols = pl.ds(pl.multiple_of(n * W, W), W)
        router = rpad[:, cols].astype(BF16)
        moe = combined(0, cols).astype(BF16).astype(F32)
        v = moe + nn(dl_hi, router) + nn(dl_lo, router)
        dm[:, cols] = v
        x = g_all[0, d, y, :, cols].astype(F32)
        gpart[d, :, cols] = jnp.sum(v * x * r_tok[:, 0:1], axis=0, keepdims=True)
        return tot + jnp.sum(v * sm[y, GAIN_ROW : GAIN_ROW + 1, cols] * x, axis=-1, keepdims=True)

    part = lax.fori_loop(0, tiles, tail_one, jnp.zeros((TOK, 1), F32))
    ip[y] = jnp.broadcast_to(part, (TOK, 128))
    for v in others_y:
        remote(ip.at[y], ip.at[y], ipbase + y, (p, d, v))
    for s in others_d:
        remote(gpart.at[d], gpart.at[d], gpbase + d, (p, s, y))
    for v in others_y:
        arrived(ip.at[v], ipbase + v)
    inner_sum = ip[0]
    for v in range(1, NY):
        inner_sum = inner_sum + ip[v]
    inner_sum = inner_sum[:, 0:1]

    def tail_two(n, c):
        cols = pl.ds(pl.multiple_of(n * W, W), W)
        r = r_tok[:, 0:1]
        h = dm[:, cols] * sm[y, GAIN_ROW : GAIN_ROW + 1, cols]
        x = g_all[0, d, y, :, cols].astype(F32)
        g = g_all[1, d, y, :, cols].astype(F32)
        ig[:, cols] = (g + r * h - x * (r * r * r) * inner_sum / D).astype(BF16)
        return c

    lax.fori_loop(0, tiles, tail_two, 0)

    def hand_on(src, dst, which, has, gets, where):
        i = counter["s"]
        counter["s"] += 1
        c = pltpu.make_async_remote_copy(
            src_ref=src, dst_ref=dst, send_sem=send_sem.at[i], recv_sem=recv_sem.at[zbase + which],
            device_id=where, device_id_type=MESH,
        )

        @pl.when(has)
        def _():
            c.start()

        @pl.when(jnp.logical_not(gets))
        def _():
            dst[...] = jnp.zeros_like(dst)

        def done():
            @pl.when(has)
            def _():
                c.wait_send()

            @pl.when(gets)
            def _():
                c.wait_recv()

        return done

    done_b = hand_on(ig, pb, 0, p > 0, p < NP - 1, (down, d, y))

    for i in range(NY):
        combine(1, i, kept_f[i])
    for w in others_y:
        arrived(comb.at[1, w], cbase[1] + w)

    def out_tile(n, c):
        cols = pl.ds(pl.multiple_of(n * W, W), W)
        fo[:, cols] = (g_all[2, d, y, :, cols].astype(F32) + combined(1, cols)).astype(BF16)
        return c

    lax.fori_loop(0, tiles, out_tile, 0)
    done_f = hand_on(fo, pf, 1, p < NP - 1, p > 0, (up, d, y))

    for s in others_d:
        arrived(gpart.at[s], gpbase + s)
    total = gpart[0]
    for s in range(1, ND):
        total = total + gpart[s]
    gg[...] = total
    for c in pending:
        c.wait_send()
    done_b()
    done_f()


def local(mesh_sizes, entering, pending, stashed_in, forward_routes, backward_routes, norm_gains, w_router, w_gateup, w_down):
    NP, ND, NY = mesh_sizes
    _, TOK, DL = entering.shape
    K = forward_routes.shape[2]
    E = w_router.shape[2]
    FFL = w_gateup.shape[4]
    D = w_gateup.shape[2]
    CAP = TOK * K // E
    assert E == ND and E <= GAIN_ROW and 2 * K <= 8 and D == DL * NY
    routes = jnp.concatenate([forward_routes[0].T, backward_routes[0].T], axis=0)
    routes = jnp.pad(routes, ((0, 8 - 2 * K), (0, 0)), constant_values=-1)
    small = jnp.concatenate(
        [w_router[0].T.astype(F32), jnp.zeros((GAIN_ROW - E, DL), F32), norm_gains[0][None]], axis=0
    )
    wgu = jnp.transpose(w_gateup[0, 0], (1, 0, 2))
    cfg = (NP, ND, NY, TOK, DL, FFL, K, E, CAP)
    NS = E * CAP
    nsend = 3 * (2 * (ND // 2 + NY) * 4 + 4 * ND * NY) + 8 * ND * NY + 64
    nrecv = 3 * ND * NY * 2 + 3 * ND * NY + 4 * ND + 6 * NY + 16
    out = jax.ShapeDtypeStruct((TOK, DL), BF16)
    V = pltpu.VMEM
    res = pl.pallas_call(
        functools.partial(kernel, cfg),
        out_shape=[out, out, out, out, jax.ShapeDtypeStruct((1, DL), F32)],
        in_specs=[pl.BlockSpec(memory_space=pl.ANY)] * 7,
        out_specs=[pl.BlockSpec(memory_space=pltpu.VMEM)] * 5,
        scratch_shapes=[
            V((3, ND, NY, TOK, DL), BF16),
            V((ND, 8, TOK), jnp.int32),
            V((NY, 8, DL), F32),
            V((2, NY, DL, FFL), BF16),
            V((NY, FFL, DL), BF16),
            V((NY, NS, DL), BF16),
            V((NY, NS, DL), BF16),
            V((NS, FFL), F32),
            V((NS, FFL), F32),
            V((NS, FFL), F32),
            V((NS, FFL), BF16),
            V((2, NS, FFL), BF16),
            V((2, NY, ND, CAP, DL), BF16),
            V((2, NY, ND, CAP, DL), BF16),
            V((2, NY, TOK, DL), BF16),
            V((2, NY, TOK, DL), BF16),
            V((TOK, DL), F32),
            V((2, E, CAP, TOK), BF16),
            V((2, 2, TOK, NS), BF16),
            V((ND, 8, CAP), F32),
            V((ND, NY, 8, CAP), F32),
            V((TOK, DL), F32),
            V((NY, TOK, 128), F32),
            V((ND, 1, DL), F32),
            V((TOK, 128), F32),
            V((TOK, DL), F32),
            pltpu.SemaphoreType.DMA((nsend,)),
            pltpu.SemaphoreType.DMA((nrecv,)),
            pltpu.SemaphoreType.DMA((64,)),
        ],
        compiler_params=pltpu.CompilerParams(
            collective_id=0, has_side_effects=True, vmem_limit_bytes=62 * 1024 * 1024
        ),
    )(stashed_in[0], pending[0], entering[0], routes, small, wgu, w_down[0, 0])
    fo, ig, pf, pb, gg = res
    return fo[None], ig[None], pf[None], pb[None], gg


def solution(mesh):
    tokens = P("pipe", "dp", "expert")
    placed = (
        tokens, tokens, tokens,
        P("pipe", "dp", None), P("pipe", "dp", None),
        P("pipe", "expert"), P("pipe", "expert", None),
        P("pipe", "dp", None, None, "expert"), P("pipe", "dp", "expert", None),
    )
    sizes = tuple(mesh.shape[a] for a in ("pipe", "dp", "expert"))
    return jax.shard_map(
        functools.partial(local, sizes),
        mesh=mesh,
        in_specs=placed,
        out_specs=(tokens, tokens, tokens, tokens, P("pipe", "expert")),
        check_vma=False,
    )
```

time: 332 us -> 190 us (0.57)
  Pallas kernels: 0 us -> 168 us
  waiting for transfers between devices: 153 us -> 0 us
  blocking collectives: 78.3 us -> 0 us
  matrix products: 30.2 us -> 0 us
  other arithmetic: 19.6 us -> 2.83 us
  starting transfers between devices: 15.6 us -> 0 us
  between operations: 14.2 us -> 0.65 us
    pallas_call x0 -> x1, Pallas kernels: none -> 168 us  [local(): pl.pallas_call(functools.partial(kernel, cfg), out_shape=[out, out, out,...]
    all_gather x3 -> x0, waiting for transfers between devices: 75.3 us -> none  [the longest x1 32.3 us: compute(): lax.all_gather(received, 'expert', axis=3, tiled=True)]
    all_to_all x3 -> x0, blocking collectives: 52.9 us -> none  [the longest x1 17.7 us: run_backward(): lax.all_to_all(row_buffer, 'dp', split_axis=0, concat_axis=0, tiled=True)]
    reduce_scatter x2 -> x0, waiting for transfers between devices: 45.9 us -> none  [compute(): lax.psum_scatter(partial_value.astype(jnp.bfloat16), 'expert', scatter_di...]
    dot_general x11 -> x0, matrix products: 30.2 us -> none  [the longest x1 7.11 us: compute(): jnp.einsum('sxckf,xdkf->sxcd', stacked, gate_up, preferred_element_type=j...]
    all_to_all x3 -> x0, waiting for transfers between devices: 27.7 us -> none  [the longest x1 12.7 us: compute(): return lax.all_to_all(summed, 'dp', split_axis=0, concat_axis=0, tiled=True)]
    psum x4 -> x0, blocking collectives: 25.4 us -> none  [the longest x3 18.9 us: feature_sum(): return lax.psum(values, 'expert')]
    unnamed x24 -> x6, local copies, waits for them, and re-layouts: 4.11 us -> 16.8 us
  transfers between devices with their start and end apart: 10 -> 0, of which waited for: 9 -> 0; matrix products, arithmetic and copies ran while one was open for 8% -> 0% of each run, Pallas kernels for 0% -> 0%
where the time goes in v1:
time: 190 us; the launch traced here: 189 us
  Pallas kernels  168 us (88%)
  local copies, waits for them, and re-layouts  17.4 us (9%)
  other arithmetic  2.83 us (1%)
    pallas_call x1, Pallas kernels, local(): pl.pallas_call(functools.partial(kernel, cfg), out_shape=[out, out, out,...  168 us
    unnamed x6, local copies, waits for them, and re-layouts  16.8 us

profile of v1, /device:TPU:0, one launch (start us, length us, event | category | flops | bytes accessed | tf_op | source)
XLA Modules:
  0.0 189.3 jit_solution(10826607795522509146)
XLA Ops:
  0.6 0.1 pad.6.clone
  0.7 0.7 pad_add_fusion
  1.4 0.6 pad.4.routes_in
  2.0 0.7 convert_bitcast_fusion
  2.7 1.4 pad_maximum_fusion.small_in
  4.1 7.9 %copy.16 = bf16[1,1,4096,2,512]{4,2,3,1,0:T(8,128)(2,1)} copy(bf16[1,1,4096,2,512]{4,3,2,1,0:T(2,128)(2,1)} %param.16) | data formatting | bytes 16777216 | tf_op args[7]
  12.1 168.4 %shard_map.128 = (bf16[128,2048]{1,0:T(8,128)(2,1)}, bf16[128,2048]{1,0:T(8,128)(2,1)}, bf16[128,2048]{1,0:T(8,128)(2,1)}, bf16[128,2048]{1,0:T(8,128)(2,1)}, f32[1,2048]{1,0:T(1,128)}) custom-call(bf16[128,2048]{1,0:T(8,128)(2,1)} %bitcast.30, bf16[128,2048]{1,0:T(8,128)(2,1)} %bitcast.31, bf16[128,2048]{1,0:T(8,128)(2,1)} %bitcast.32, ...), custom_call_target="tpu_custom_call" | custom-call | tf_op jit(solution)/shard_map/pallas_call | solution.py:514
  180.5 1.9 copy.22
  182.3 1.9 copy.23
  184.2 1.9 copy.24
  186.1 1.9 copy.25
  188.0 1.3 copy.26
  (1 shorter events, 0.0 us)

commit v2 on v1

--- a/solution.py
+++ b/solution.py
@@ -29,18 +29,40 @@
     return hi, (v - hi.astype(F32)).astype(BF16)
 
 
+def settle(*refs):
+    sources, targets, held, sem = refs[:5], refs[5:10], refs[10:15], refs[15]
+    into = [pltpu.make_async_copy(a, b, sem.at[i]) for i, (a, b) in enumerate(zip(sources, held))]
+    out = [pltpu.make_async_copy(a, b, sem.at[5 + i]) for i, (a, b) in enumerate(zip(held, targets))]
+    for c in into:
+        c.start()
+    for a, b in zip(into, out):
+        a.wait()
+        b.start()
+    for c in out:
+        c.wait()
+
+
+def lanes(v):
+    total = v[:, 0:128]
+    for i in range(1, v.shape[1] // 128):
+        total = total + v[:, i * 128 : (i + 1) * 128]
+    return total
+
+
 def kernel(
     cfg,
-    xb_in, gy_in, xf_in, routes_in, small_in, wgu_in, wd_in,
+    xb_in, gy_in, xf_in, wgu_in, wd_in, fr_in, br_in, router_in, gain_in,
     fo, ig, pf, pb, gg,
     g_all, rt, sm, wgu, wd, rows_x, rows_g, acc_a, acc_b, acc_w, inner, grad,
-    ret_send, ret, comb_send, comb, own, hot, wts, gs, gr, dm, ip, gpart, r_tok, rpad,
+    ret_send, ret, comb_send, comb, own, hot, wts, gs, gr, dm, ip, gpart, r_tok, rpad, r_row,
     send_sem, recv_sem, local_sem,
 ):
     NP, ND, NY, TOK, DL, FFL, K, E, CAP = cfg
     HT = TOK // 2
     W = min(256, DL)
     tiles = DL // W
+    BW = min(512, DL // 2)
+    HALF = DL // 2
     NSLOT = E * CAP
     D = DL * NY
     p, d, y = lax.axis_index("pipe"), lax.axis_index("dp"), lax.axis_index("expert")
@@ -83,8 +105,12 @@
         return base
 
     first = [local(src, g_all.at[t, d, y]) for t, src in enumerate((xb_in, gy_in, xf_in))]
-    first.append(local(routes_in, rt.at[d]))
-    first.append(local(small_in, sm.at[y]))
+    rt[d] = jnp.full((8, TOK), -1, jnp.int32)
+    rt[d, 0:K, :] = fr_in[...]
+    rt[d, K : 2 * K, :] = br_in[...]
+    sm[y] = jnp.zeros((8, DL), F32)
+    sm[y, 0:E, :] = router_in[...].astype(F32)
+    sm[y, GAIN_ROW : GAIN_ROW + 1, :] = gain_in[...]
     weights = [local(wgu_in.at[k, pl.ds(j * DL, DL)], wgu.at[k, j]) for k in range(2) for j in range(NY)]
     weights += [local(wd_in.at[:, pl.ds(j * DL, DL)], wd.at[j]) for j in range(NY)]
 
@@ -181,28 +207,23 @@
         return one_hot(member[0:1, :], pos[0:1, :]).astype(BF16)
 
     def dispatch(t, base, rows, scaled):
+        PW = min(512, DL)
+
         def body(s, _):
             pick = expert_hot(s, base)
             where = pl.ds(pl.multiple_of(s * CAP, CAP), CAP)
-            total = jnp.zeros((CAP, 1), F32)
+            total = jnp.zeros((CAP, 128), F32)
             for j in range(NY):
-                def step(i, tot, j=j):
-                    cols = pl.ds(pl.multiple_of(i * W, W), W)
+                for i in range(DL // PW):
+                    cols = pl.ds(i * PW, PW)
                     part = nn(pick, g_all[t, s, j, :, cols])
+                    if scaled:
+                        total = total + lanes(part * part)
+                        part = part * sm[j, GAIN_ROW : GAIN_ROW + 1, cols]
                     rows[j, where, cols] = part.astype(BF16)
-                    return tot + jnp.sum(part * part, axis=-1, keepdims=True)
-
-                total = lax.fori_loop(0, tiles, step, total)
             if scaled:
-                scaling = lax.rsqrt(total / D + EPSILON)
-                for j in range(NY):
-                    def norm(i, c, j=j):
-                        cols = pl.ds(pl.multiple_of(i * W, W), W)
-                        v = rows[j, where, cols].astype(F32) * scaling * sm[j, GAIN_ROW : GAIN_ROW + 1, cols]
-                        rows[j, where, cols] = v.astype(BF16)
-                        return c
-
-                    lax.fori_loop(0, tiles, norm, 0)
+                scaling = lax.rsqrt(jnp.sum(total, axis=-1, keepdims=True) / D + EPSILON)
+                r_row[where, :] = jnp.broadcast_to(scaling, (CAP, 128))
             return 0
 
         lax.fori_loop(0, ND, body, 0)
@@ -210,7 +231,7 @@
     def project_up():
         acc_a[...] = jnp.zeros_like(acc_a)
         acc_b[...] = jnp.zeros_like(acc_b)
-        KT = min(512, DL)
+        KT = min(1024, DL)
         for j in range(NY):
             def body(i, c, j=j):
                 ks = pl.ds(pl.multiple_of(i * KT, KT), KT)
@@ -223,7 +244,7 @@
 
     def project_w():
         acc_w[...] = jnp.zeros_like(acc_w)
-        KT = min(512, DL)
+        KT = min(1024, DL)
         for j in range(NY):
             def body(i, c, j=j):
                 ks = pl.ds(pl.multiple_of(i * KT, KT), KT)
@@ -236,11 +257,12 @@
         def squares(j, tot):
             def step(i, tt):
                 v = g_all[t, d, j, :, pl.ds(pl.multiple_of(i * W, W), W)].astype(F32)
-                return tt + jnp.sum(v * v, axis=-1, keepdims=True)
-
-            return lax.fori_loop(0, tiles, step, tot)
-
-        total = lax.fori_loop(0, NY, squares, jnp.zeros((TOK, 1), F32))
+                return tt + lanes(v * v)
+
+            return lax.fori_loop(0, tiles, step, tot, unroll=2)
+
+        total = lax.fori_loop(0, NY, squares, jnp.zeros((TOK, 128), F32))
+        total = jnp.sum(total, axis=-1, keepdims=True)
         scaling = lax.rsqrt(total / D + EPSILON)
 
         def logit(j, acc):
@@ -249,7 +271,7 @@
                 v = g_all[t, d, j, :, cols].astype(F32) * scaling * sm[j, GAIN_ROW : GAIN_ROW + 1, cols]
                 return a + nt(sm[j, :, cols].astype(BF16), v.astype(BF16))
 
-            return lax.fori_loop(0, tiles, step, acc)
+            return lax.fori_loop(0, tiles, step, acc, unroll=2)
 
         logits = lax.fori_loop(0, NY, logit, jnp.zeros((8, TOK), F32))
         picks = rt[d]
@@ -271,35 +293,38 @@
         wts[u, 1] = lo
         return scaling, sel, sg, total_sg
 
-    retbase = [block(NY * ND) for _ in range(2)]
-    cbase = [block(NY) for _ in range(2)]
-    gcbase, ipbase, gpbase, zbase = block(ND * NY), block(NY), block(ND), block(2)
+    retbase = [block(NY * ND * 2) for _ in range(2)]
+    cbase = [block(2 * NY) for _ in range(2)]
+    gcbase, ipbase, gpbase, zbase = block(ND * NY), block(NY), block(ND), block(3)
 
     def chunk_of(i):
         return lax.rem(y + 1 + i, NY)
 
-    def produce(u, i, make):
+    def back(ref, u, j, s, h):
+        return ref.at[u, j, s, :, pl.ds(h * HALF, HALF)]
+
+    def produce(u, i, h, make):
         j = chunk_of(i)
 
         def body(n, c):
-            cols = pl.ds(pl.multiple_of(n * W, W), W)
-            ret_send[u, j, :, :, cols] = make(j, cols).astype(BF16).reshape(ND, CAP, W)
+            cols = pl.ds(pl.multiple_of(h * HALF + n * BW, BW), BW)
+            ret_send[u, j, :, :, cols] = make(j, cols).astype(BF16).reshape(ND, CAP, BW)
             return c
 
-        lax.fori_loop(0, tiles, body, 0)
+        lax.fori_loop(0, HALF // BW, body, 0, unroll=True)
         for s in others_d:
-            remote(ret_send.at[u, j, s], ret.at[u, j, d], retbase[u] + j * ND + d, (p, s, y))
-        return local(ret_send.at[u, j, d], ret.at[u, j, d])
-
-    def combine(u, i, kept):
+            remote(back(ret_send, u, j, s, h), back(ret, u, j, d, h), retbase[u] + (j * ND + d) * 2 + h, (p, s, y))
+        return local(back(ret_send, u, j, d, h), back(ret, u, j, d, h))
+
+    def combine(u, i, h, kept):
         j = chunk_of(i)
         for s in others_d:
-            arrived(ret.at[u, j, s], retbase[u] + j * ND + s)
+            arrived(back(ret, u, j, s, h), retbase[u] + (j * ND + s) * 2 + h)
         kept.wait()
 
         def body(n, c):
-            cols = pl.ds(pl.multiple_of(n * W, W), W)
-            r = ret[u, j, :, :, cols].reshape(NSLOT, W)
+            cols = pl.ds(pl.multiple_of(h * HALF + n * BW, BW), BW)
+            r = ret[u, j, :, :, cols].reshape(NSLOT, BW)
             v = nn(wts[u, 0], r) + nn(wts[u, 1], r)
             if i < NY - 1:
                 comb_send[u, j, :, cols] = v.astype(BF16)
@@ -307,9 +332,14 @@
                 own[:, cols] = v
             return c
 
-        lax.fori_loop(0, tiles, body, 0)
+        lax.fori_loop(0, HALF // BW, body, 0, unroll=True)
         if i < NY - 1:
-            remote(comb_send.at[u, j], comb.at[u, y], cbase[u] + y, (p, d, j))
+            cols = pl.ds(h * HALF, HALF)
+            remote(comb_send.at[u, j, :, cols], comb.at[u, y, :, cols], cbase[u] + y * 2 + h, (p, d, j))
+
+    def comb_arrived(u, h):
+        for w in others_y:
+            arrived(comb.at[u, w, :, pl.ds(h * HALF, HALF)], cbase[u] + w * 2 + h)
 
     def combined(u, cols):
         v = own[:, cols]
@@ -334,7 +364,8 @@
 
     def activate(s, c):
         where = pl.ds(pl.multiple_of(s * CAP, CAP), CAP)
-        a, b, w = acc_a[where, :], acc_b[where, :], acc_w[where, :]
+        r = r_row[where, 0:1]
+        a, b, w = acc_a[where, :] * r, acc_b[where, :] * r, acc_w[where, :]
         sa = jax.nn.sigmoid(a)
         act = a * sa
         prod = (act * b).astype(BF16).astype(F32) * w
@@ -355,10 +386,10 @@
     def back_rows(j, cols):
         return nt(grad[0], wgu[0, j, cols, :]) + nt(grad[1], wgu[1, j, cols, :])
 
-    relayed = False
-    kept_b = []
+    kept_b, kept_f = {}, {}
     for i in range(NY):
-        kept_b.append(produce(0, i, back_rows))
+        for h in range(2):
+            kept_b[i, h] = produce(0, i, h, back_rows)
         if i == 0:
             relay(2)
     owner(2, 0, 1)
@@ -368,7 +399,8 @@
 
     def act_forward(s, c):
         where = pl.ds(pl.multiple_of(s * CAP, CAP), CAP)
-        a, b = acc_a[where, :], acc_b[where, :]
+        r = r_row[where, 0:1]
+        a, b = acc_a[where, :] * r, acc_b[where, :] * r
         inner[where, :] = (a * jax.nn.sigmoid(a) * b).astype(BF16)
         return c
 
@@ -377,10 +409,12 @@
     def forward_rows(j, cols):
         return nn(inner[...], wd[j, :, cols])
 
-    kept_f = []
     for i in range(NY):
-        combine(0, i, kept_b[i])
-        kept_f.append(produce(1, i, forward_rows))
+        for h in range(2):
+            kept_f[i, h] = produce(1, i, h, forward_rows)
+    for i in range(NY):
+        for h in range(2):
+            combine(0, i, h, kept_b[i, h])
 
     kept_gc.wait()
     for o in range(ND):
@@ -399,8 +433,8 @@
     dl_hi, dl_lo = split(jnp.transpose(jnp.concatenate([dl, jnp.zeros((TOK - 8, TOK), F32)], axis=0)))
     rpad[...] = jnp.zeros_like(rpad)
     rpad[0:8, :] = sm[y]
-    for w in others_y:
-        arrived(comb.at[0, w], cbase[0] + w)
+    for h in range(2):
+        comb_arrived(0, h)
 
     def tail_one(n, tot):
         cols = pl.ds(pl.multiple_of(n * W, W), W)
@@ -465,18 +499,22 @@
 
     done_b = hand_on(ig, pb, 0, p > 0, p < NP - 1, (down, d, y))
 
-    for i in range(NY):
-        combine(1, i, kept_f[i])
-    for w in others_y:
-        arrived(comb.at[1, w], cbase[1] + w)
-
-    def out_tile(n, c):
-        cols = pl.ds(pl.multiple_of(n * W, W), W)
-        fo[:, cols] = (g_all[2, d, y, :, cols].astype(F32) + combined(1, cols)).astype(BF16)
-        return c
-
-    lax.fori_loop(0, tiles, out_tile, 0)
-    done_f = hand_on(fo, pf, 1, p < NP - 1, p > 0, (up, d, y))
+    for i in range(NY - 1):
+        for h in range(2):
+            combine(1, i, h, kept_f[i, h])
+    done_f = []
+    for h in range(2):
+        combine(1, NY - 1, h, kept_f[NY - 1, h])
+        comb_arrived(1, h)
+
+        def out_tile(n, c):
+            cols = pl.ds(pl.multiple_of(h * HALF + n * BW, BW), BW)
+            fo[:, cols] = (g_all[2, d, y, :, cols].astype(F32) + combined(1, cols)).astype(BF16)
+            return c
+
+        lax.fori_loop(0, HALF // BW, out_tile, 0)
+        half = pl.ds(h * HALF, HALF)
+        done_f.append(hand_on(fo.at[:, half], pf.at[:, half], 1 + h, p < NP - 1, p > 0, (up, d, y)))
 
     for s in others_d:
         arrived(gpart.at[s], gpbase + s)
@@ -487,7 +525,8 @@
     for c in pending:
         c.wait_send()
     done_b()
-    done_f()
+    for done in done_f:
+        done()
 
 
 def local(mesh_sizes, entering, pending, stashed_in, forward_routes, backward_routes, norm_gains, w_router, w_gateup, w_down):
@@ -499,22 +538,17 @@
     D = w_gateup.shape[2]
     CAP = TOK * K // E
     assert E == ND and E <= GAIN_ROW and 2 * K <= 8 and D == DL * NY
-    routes = jnp.concatenate([forward_routes[0].T, backward_routes[0].T], axis=0)
-    routes = jnp.pad(routes, ((0, 8 - 2 * K), (0, 0)), constant_values=-1)
-    small = jnp.concatenate(
-        [w_router[0].T.astype(F32), jnp.zeros((GAIN_ROW - E, DL), F32), norm_gains[0][None]], axis=0
-    )
     wgu = jnp.transpose(w_gateup[0, 0], (1, 0, 2))
     cfg = (NP, ND, NY, TOK, DL, FFL, K, E, CAP)
     NS = E * CAP
-    nsend = 3 * (2 * (ND // 2 + NY) * 4 + 4 * ND * NY) + 8 * ND * NY + 64
-    nrecv = 3 * ND * NY * 2 + 3 * ND * NY + 4 * ND + 6 * NY + 16
+    nsend = 3 * (2 * (ND // 2 + NY) * 4 + 4 * ND * NY) + 12 * ND * NY + 64
+    nrecv = 3 * ND * NY * 2 + 5 * ND * NY + 4 * ND + 8 * NY + 16
     out = jax.ShapeDtypeStruct((TOK, DL), BF16)
     V = pltpu.VMEM
     res = pl.pallas_call(
         functools.partial(kernel, cfg),
         out_shape=[out, out, out, out, jax.ShapeDtypeStruct((1, DL), F32)],
-        in_specs=[pl.BlockSpec(memory_space=pl.ANY)] * 7,
+        in_specs=[pl.BlockSpec(memory_space=pl.ANY)] * 5 + [pl.BlockSpec(memory_space=pltpu.VMEM)] * 4,
         out_specs=[pl.BlockSpec(memory_space=pltpu.VMEM)] * 5,
         scratch_shapes=[
             V((3, ND, NY, TOK, DL), BF16),
@@ -543,6 +577,7 @@
             V((ND, 1, DL), F32),
             V((TOK, 128), F32),
             V((TOK, DL), F32),
+            V((NS, 128), F32),
             pltpu.SemaphoreType.DMA((nsend,)),
             pltpu.SemaphoreType.DMA((nrecv,)),
             pltpu.SemaphoreType.DMA((64,)),
@@ -550,8 +585,17 @@
         compiler_params=pltpu.CompilerParams(
             collective_id=0, has_side_effects=True, vmem_limit_bytes=62 * 1024 * 1024
         ),
-    )(stashed_in[0], pending[0], entering[0], routes, small, wgu, w_down[0, 0])
-    fo, ig, pf, pb, gg = res
+    )(
+        stashed_in[0], pending[0], entering[0], wgu, w_down[0, 0],
+        forward_routes[0].T, backward_routes[0].T, w_router[0].T, norm_gains,
+    )
+    fo, ig, pf, pb, gg = pl.pallas_call(
+        settle,
+        out_shape=[jax.ShapeDtypeStruct(v.shape, v.dtype) for v in res],
+        in_specs=[pl.BlockSpec(memory_space=pl.ANY)] * 5,
+        out_specs=[pl.BlockSpec(memory_space=pl.ANY)] * 5,
+        scratch_shapes=[V(v.shape, v.dtype) for v in res] + [pltpu.SemaphoreType.DMA((10,))],
+    )(*res)
     return fo[None], ig[None], pf[None], pb[None], gg
 
 

time: 190 us -> 136 us (0.72)
  Pallas kernels: 168 us -> 127 us
  local copies, waits for them, and re-layouts: 17.4 us -> 7.94 us
  other arithmetic: 2.83 us -> 0 us
    pallas_call x1, Pallas kernels: 168 us -> 125 us  [local(): pl.pallas_call(functools.partial(kernel, cfg), out_shape=[out, out, out,...]
    unnamed x6 -> x1, local copies, waits for them, and re-layouts: 16.8 us -> 7.94 us
    pallas_call x0 -> x1, Pallas kernels: none -> 2.44 us  [local(): pl.pallas_call(settle, out_shape=[jax.ShapeDtypeStruct(v.shape, v.dtype)...]
    concatenate x2 -> x0, other arithmetic: 2.1 us -> none  [the longest x1 1.4 us: local(): jnp.concatenate([w_router[0].T.astype(F32), jnp.zeros((GAIN_ROW - E, DL),...]
where the time goes in v2:
time: 136 us
  Pallas kernels  127 us (93%)
  local copies, waits for them, and re-layouts  7.94 us (6%)
    pallas_call x1, Pallas kernels, local(): pl.pallas_call(functools.partial(kernel, cfg), out_shape=[out, out, out,...  125 us
    unnamed x1, local copies, waits for them, and re-layouts  7.94 us

profile of v2, /device:TPU:0, one launch (start us, length us, event | category | flops | bytes accessed | tf_op | source)
XLA Modules:
  0.0 135.9 jit_solution(10379617985212482297)
XLA Ops:
  0.6 7.9 %copy.16 = bf16[1,1,4096,2,512]{4,2,3,1,0:T(8,128)(2,1)} copy(bf16[1,1,4096,2,512]{4,3,2,1,0:T(2,128)(2,1)} %param.16) | data formatting | bytes 16777216 | tf_op args[7]
  8.6 124.9 %shard_map.128 = (bf16[128,2048]{1,0:T(8,128)(2,1)}, bf16[128,2048]{1,0:T(8,128)(2,1)}, bf16[128,2048]{1,0:T(8,128)(2,1)}, bf16[128,2048]{1,0:T(8,128)(2,1)}, f32[1,2048]{1,0:T(1,128)}) custom-call(bf16[128,2048]{1,0:T(8,128)(2,1)} %bitcast.24, bf16[128,2048]{1,0:T(8,128)(2,1)} %bitcast.25, bf16[128,2048]{1,0:T(8,128)(2,1)} %bitcast.26, ...), custom_call_target="tpu_custom_call" | custom-call | tf_op jit(solution)/shard_map/pallas_call | solution.py:548
  133.4 2.4 %shard_map.129 = (bf16[128,2048]{1,0:T(8,128)(2,1)}, bf16[128,2048]{1,0:T(8,128)(2,1)}, bf16[128,2048]{1,0:T(8,128)(2,1)}, bf16[128,2048]{1,0:T(8,128)(2,1)}, f32[1,2048]{1,0:T(1,128)}) custom-call(bf16[128,2048]{1,0:T(8,128)(2,1)} %get-tuple-element.15.refs_0_, bf16[128,2048]{1,0:T(8,128)(2,1)} %get-tuple-element.16.refs_1_, ...), custom_call_target="tpu_custom_call" | custom-call | tf_op jit(solution)/shard_map/pallas_call | solution.py:592

commit v3 on v2

--- a/solution.py
+++ b/solution.py
@@ -155,13 +155,13 @@
         for i in range(2):
             for x in across:
                 gwait(t, x, y, i)
-                if i == 0:
+                if i == 0 or t == 2:
                     for v in others_y:
-                        gsend(t, x, y, 0, (p, d, v))
+                        gsend(t, x, y, i, (p, d, v))
                 gsend(t, x, y, i, (p, mate, y))
             for v in others_y:
                 gwait(t, d, v, 1 - i)
-                if i == 0:
+                if i == 0 and t < 2:
                     for x in across:
                         gsend(t, d, v, 1, (p, x, y))
                 gsend(t, d, v, 1 - i, (p, mate, y))

time: 136 us -> 130 us (0.956)
  Pallas kernels: 127 us -> 121 us
    pallas_call x1, Pallas kernels: 125 us -> 118 us  [local(): pl.pallas_call(functools.partial(kernel, cfg), out_shape=[out, out, out,...]
where the time goes in v3:
time: 130 us; the launch traced here: 129 us
  Pallas kernels  121 us (93%)
  local copies, waits for them, and re-layouts  7.94 us (6%)
    pallas_call x1, Pallas kernels, local(): pl.pallas_call(functools.partial(kernel, cfg), out_shape=[out, out, out,...  118 us
    unnamed x1, local copies, waits for them, and re-layouts  7.94 us

profile of v3, /device:TPU:0, one launch (start us, length us, event | category | flops | bytes accessed | tf_op | source)
XLA Modules:
  0.0 129.2 jit_solution(5911328297040909815)
XLA Ops:
  0.6 7.9 %copy.16 = bf16[1,1,4096,2,512]{4,2,3,1,0:T(8,128)(2,1)} copy(bf16[1,1,4096,2,512]{4,3,2,1,0:T(2,128)(2,1)} %param.16) | data formatting | bytes 16777216 | tf_op args[7]
  8.6 118.2 %shard_map.128 = (bf16[128,2048]{1,0:T(8,128)(2,1)}, bf16[128,2048]{1,0:T(8,128)(2,1)}, bf16[128,2048]{1,0:T(8,128)(2,1)}, bf16[128,2048]{1,0:T(8,128)(2,1)}, f32[1,2048]{1,0:T(1,128)}) custom-call(bf16[128,2048]{1,0:T(8,128)(2,1)} %bitcast.24, bf16[128,2048]{1,0:T(8,128)(2,1)} %bitcast.25, bf16[128,2048]{1,0:T(8,128)(2,1)} %bitcast.26, ...), custom_call_target="tpu_custom_call" | custom-call | tf_op jit(solution)/shard_map/pallas_call | solution.py:548
  126.8 2.4 %shard_map.129 = (bf16[128,2048]{1,0:T(8,128)(2,1)}, bf16[128,2048]{1,0:T(8,128)(2,1)}, bf16[128,2048]{1,0:T(8,128)(2,1)}, bf16[128,2048]{1,0:T(8,128)(2,1)}, f32[1,2048]{1,0:T(1,128)}) custom-call(bf16[128,2048]{1,0:T(8,128)(2,1)} %get-tuple-element.15.refs_0_, bf16[128,2048]{1,0:T(8,128)(2,1)} %get-tuple-element.16.refs_1_, ...), custom_call_target="tpu_custom_call" | custom-call | tf_op jit(solution)/shard_map/pallas_call | solution.py:592
